TPU v7x, 32 devices: a whole 2x2x4 slice. The times are simulated.
32 devices in a mesh: dp: 2 (over y), row: 4 (over x, core), col: 4 (over z).
Axes of the slice: x: 2, y: 2, z: 4, core: 2. Of those that a mesh axis runs over, the one named last changes fastest.
Arguments:
- tokens: bfloat16 [2048, 8192], P(('dp', 'col'), 'row'), may hold values from -6 to 6
- frozen_weight: bfloat16 [8192, 8192], P('row', 'col'), may hold values from -0.0625 to 0.0625
- input_adapter_factor: bfloat16 [16, 8192], P(None, 'row'), may hold values from -0.0625 to 0.0625
- output_adapter_factor: bfloat16 [16, 8192], P(None, 'col'), may hold values from -1.5 to 1.5
- magnitude: float32 [8192], P('col'), may hold values from 0.5 to 2
- cotangent: bfloat16 [2048, 8192], P(('dp', 'row'), 'col'), may hold values from -6 to 6
- sequence_lengths: int32 [2, 8], P('dp'), may hold values from 1 to 512, 1024 in all within a row
Outputs:
- projected: bfloat16 [2048, 8192], P(('dp', 'row'), 'col')
- grad_mag: float32 [8192], P('col')
- input_factor_gradient: float32 [16, 8192], P(None, 'row')
- grad_b: float32 [16, 8192], P(None, 'col')
Inputs may be any that keep to these rules, and one draw needn't show every extreme that they name: `sequence_lengths`: each group's 8 lengths sum to 1024, and one of them is exactly 512.
All inputs are finite; a program needn't handle non-finite values.
Results may differ from a plain program's by a relative error of at most 0.0052.
Values may be sent and summed in bfloat16 or wider, within the bound.
No kernel may reach another device: no remote copies, remote signals or barrier semaphores. Data moves between devices by JAX's collectives and lax.ppermute only.
A program may use at most 64 MiB of HBM per device.

v0:
```python
import jax
import jax.numpy as jnp
from jax import lax
from jax.sharding import PartitionSpec as P

norm_eps = 1e-06
highest_precision = lax.Precision.HIGHEST


def contract_product(left, right, left_dim, right_dim):
    return lax.dot_general(
        left, right, (((left_dim,), (right_dim,)), ((), ())), preferred_element_type=jnp.float32
    )


def per_device(
    tokens,
    frozen_weight,
    input_adapter_factor,
    output_adapter_factor,
    magnitude,
    cotangent,
    sequence_lengths,
):
    row_count = lax.axis_size("row")
    col_count = lax.axis_size("col")
    row_index = lax.axis_index("row")
    col_index = lax.axis_index("col")
    group_index = lax.axis_index("dp")
    local_rows = tokens.shape[0]
    group_rows = local_rows * col_count
    block_rows = group_rows // row_count
    adapter_rank_size = input_adapter_factor.shape[0]
    low_rank_update = contract_product(input_adapter_factor, output_adapter_factor, 0, 0)
    merged = frozen_weight.astype(jnp.float32) + low_rank_update
    norm_terms = jnp.sum(merged * merged, axis=0)
    gram_partial_terms = contract_product(input_adapter_factor, input_adapter_factor, 1, 1)
    merged_factor_terms = jnp.dot(
        input_adapter_factor, frozen_weight, preferred_element_type=jnp.float32
    ) + jnp.dot(
        gram_partial_terms, output_adapter_factor.astype(jnp.float32), precision=highest_precision
    )
    portion = lax.all_gather(tokens, "col", axis=0, tiled=True)
    base_piece = jnp.dot(portion, frozen_weight, preferred_element_type=jnp.float32)
    down_portion = contract_product(portion, input_adapter_factor, 1, 1)
    frozen_rows, down_rows = (
        lax.psum_scatter(base_piece, "row", scatter_dimension=0, tiled=True),
        lax.psum_scatter(down_portion, "row", scatter_dimension=0, tiled=True),
    )
    norm_sq, merged_input_factor = lax.psum((norm_terms, merged_factor_terms), "row")
    down_activations = down_rows.astype(jnp.bfloat16)
    col_norm = jnp.sqrt(norm_sq + norm_eps)
    col_scale = magnitude / col_norm
    query_projection = frozen_rows + jnp.dot(
        down_activations, output_adapter_factor, preferred_element_type=jnp.float32
    )
    projected = (query_projection * col_scale[None, :]).astype(jnp.bfloat16)
    lengths = sequence_lengths[0]
    ends = jnp.cumsum(lengths, dtype=jnp.int32)
    starts = ends - lengths
    positions = row_index * block_rows + jnp.arange(block_rows, dtype=jnp.int32)
    inside = (positions[:, None] >= starts[None, :]) & (positions[:, None] < ends[None, :])
    inverse = 1.0 / lengths.astype(jnp.float32)
    weights = jnp.sum(jnp.where(inside, inverse[None, :], jnp.float32(0.0)), axis=1)
    grad_out = cotangent.astype(jnp.float32) * weights[:, None]
    scale_terms = jnp.sum(grad_out * query_projection, axis=0)
    projection_gradient = (grad_out * col_scale[None, :]).astype(jnp.bfloat16)
    bgrad_terms = contract_product(down_activations, projection_gradient, 0, 0)
    scale_grad, bgrad_data = lax.psum((scale_terms, bgrad_terms), ("dp", "row"))
    grad_mag = scale_grad / col_norm
    norm_coefficient = -scale_grad * magnitude / (col_norm * col_norm * col_norm)
    grad_b = bgrad_data + merged_input_factor * norm_coefficient[None, :]
    backward_terms = contract_product(projection_gradient, output_adapter_factor, 1, 1)
    padded = lax.dynamic_update_slice_in_dim(
        jnp.zeros((group_rows, adapter_rank_size), jnp.float32),
        backward_terms,
        row_index * block_rows,
        0,
    )
    backward_rows = lax.psum(padded, ("row", "col")).astype(jnp.bfloat16)
    back_mine = lax.dynamic_slice_in_dim(backward_rows, col_index * local_rows, local_rows, 0)
    row_term = contract_product(back_mine, tokens, 0, 0)
    scaled_output_factor = (
        output_adapter_factor.astype(jnp.float32) * norm_coefficient[None, :]
    ).astype(jnp.bfloat16)
    norm_term = contract_product(scaled_output_factor, frozen_weight, 1, 1) + jnp.dot(
        contract_product(scaled_output_factor, output_adapter_factor, 1, 1),
        input_adapter_factor.astype(jnp.float32),
        precision=highest_precision,
    )
    first_group = (group_index == 0).astype(jnp.float32)
    input_factor_gradient = lax.psum(row_term + first_group * norm_term, ("dp", "col"))
    return (projected, grad_mag, input_factor_gradient, grad_b)


def solution(mesh):
    in_specs = (
        P(("dp", "col"), "row"),
        P("row", "col"),
        P(None, "row"),
        P(None, "col"),
        P("col"),
        P(("dp", "row"), "col"),
        P("dp", None),
    )
    out_specs = (P(("dp", "row"), "col"), P("col"), P(None, "row"), P(None, "col"))
    return jax.shard_map(
        per_device, mesh=mesh, in_specs=in_specs, out_specs=out_specs, check_vma=False
    )
```

profile of v0, /device:TPU:0, one launch (start us, length us, event | category | flops | bytes accessed | tf_op | source)
XLA Modules:
  0.0 366.2 jit_solution(13270679273868545477)
XLA Ops:
  7.2 0.0 copy-start
  7.2 0.0 all-gather.2.cloned.1.call-start
  7.2 0.7 all-gather.2.cloned.1.call-update
  7.9 0.0 reduce-scatter.5.cloned.1.call-start
  8.0 85.1 %all-gather.2.cloned.1.call-done = bf16[1024,2048]{1,0:T(8,128)(2,1)} async-done(((bf16[256,2048]{1,0:T(8,128)(2,1)}), bf16[1024,2048]{1,0:T(8,128)(2,1)}) %all-gather.2.cloned.1.call-update) | async-done | bytes 4194320 | tf_op jit(solution)/shard_map/all_gather | solution.py:43
  93.1 0.0 copy-done
  93.1 4.0 %fusion.14 = f32[1024,16]{0,1:T(8,128)} fusion(bf16[1024,2048]{1,0:T(8,128)(2,1)} %all-gather.2.cloned.1.call-done, bf16[16,2048]{1,0:T(8,128)(2,1)S(1)} %copy-done), kind=kOutput, calls=%fused_computation.33 | convolution fusion | flops 67108864 | bytes 4325376 | tf_op jit(solution)/shard_map/dot_general | solution.py:11
  97.1 0.0 reduce-scatter.5.cloned.1.call-update
  97.1 0.0 reduce-scatter.3.cloned.1.call-start
  97.1 14.4 %fusion.13 = f32[1024,2048]{1,0:T(8,128)} fusion(bf16[1024,2048]{1,0:T(8,128)(2,1)} %all-gather.2.cloned.1.call-done, bf16[2048,2048]{1,0:T(8,128)(2,1)} %param.8), kind=kOutput, calls=%fused_computation.32 | convolution fusion | flops 8589934592 | bytes 20971520 | tf_op jit(solution)/shard_map/dot_general | solution.py:44
  111.6 0.0 reduce-scatter.3.cloned.1.call-update
  111.6 0.0 all-reduce.8.cloned.1.call-start
  111.6 0.1 fusion.16
  111.8 0.0 copy-start.2
  111.8 4.6 %fusion.15 = f32[16,2048]{1,0:T(8,128)S(1)} fusion(bf16[16,2048]{1,0:T(8,128)(2,1)S(1)} %copy-done, bf16[2048,2048]{1,0:T(8,128)(2,1)} %param.8), kind=kOutput, calls=%fused_computation.34 | convolution fusion | flops 134217728 | bytes 8585216 | tf_op jit(solution)/shard_map/dot_general | solution.py:38
  116.4 0.0 copy-done.2
  116.4 0.9 convolution_add_fusion.1
  117.3 0.0 all-reduce.8.cloned.1.call-update
  117.3 0.0 all-reduce.6.cloned.1.call-start
  117.3 0.0 copy-start.5
  117.4 0.0 copy-start.4
  117.4 0.0 copy-start.3
  117.4 5.9 %multiply_reduce_fusion = f32[2048]{0:T(1024)S(1)} fusion(bf16[2048,2048]{1,0:T(8,128)(2,1)} %param.8, bf16[16,2048]{1,0:T(8,128)(2,1)S(1)} %copy-done, bf16[16,2048]{1,0:T(8,128)(2,1)S(1)} %copy-done.2), kind=kOutput, calls=%fused_computation | convolution fusion | flops 150992896 | bytes 8527872 | tf_op jit(solution)/shard_map/dot_general | solution.py:11
  123.3 0.0 copy-done.5
  123.3 0.2 reduce-window.4
  123.5 6.5 %psum.42 = f32[2048]{0:T(1024)S(1)} all-reduce(f32[2048]{0:T(1024)S(1)} %multiply_reduce_fusion), channel_id=1, replica_groups=mesh['dp'=2,'row'=4,'col'=4] {'row'}, use_global_device_ids=true, to_apply=%region_3.0 | all-reduce | flops 2048 | bytes 16384 | tf_op jit(solution)/shard_map/psum | solution.py:50
  130.0 0.0 copy-done.4
  130.1 0.1 select_reduce_fusion
  130.2 0.0 copy-done.3
  130.2 0.5 convolution_dynamic-update-slice_fusion
  130.7 69.2 %psum.44 = bf16[1024,16]{1,0:T(8,128)(2,1)S(1)} all-reduce(f32[1024,16]{1,0:T(8,128)S(1)} %convolution_dynamic-update-slice_fusion), channel_id=1, replica_groups=mesh['dp'=2,'row'=4,'col'=4] {'row','col'}, use_global_device_ids=true, to_apply=%region_8.9 | all-reduce | flops 16384 | bytes 98304 | tf_op jit(solution)/shard_map/psum | solution.py:80
  199.9 0.0 reduce-scatter.5.cloned.1.call-done
  200.0 1.8 fusion.1
  201.8 0.0 all-reduce.6.cloned.1.call-update
  201.8 0.0 all-reduce.4.cloned.1.call-start
  201.8 0.0 reduce-scatter.3.cloned.1.call-done
  201.9 3.2 multiply_reduce_fusion.1
  205.1 12.1 %psum.43 = f32[2048]{0:T(1024)S(1)} all-reduce(f32[2048]{0:T(1024)S(1)} %get-tuple-element.4), channel_id=1, replica_groups=mesh['dp'=2,'row'=4,'col'=4] {'dp','row'}, use_global_device_ids=true, to_apply=%region_7.8 | all-reduce | flops 2048 | bytes 16384 | tf_op jit(solution)/shard_map/psum | solution.py:69
  217.1 0.6 fusion.6
  217.8 0.0 copy-start.1
  217.8 5.7 %fusion.3 = f32[16,2048]{1,0:T(8,128)S(1)} fusion(bf16[2048,2048]{1,0:T(8,128)(2,1)} %param.8, bf16[16,2048]{1,0:T(8,128)(2,1)S(1)} %copy-done.2, f32[2048]{0:T(1024)S(1)} %get-tuple-element.6), kind=kOutput, calls=%fused_computation.16 | convolution fusion | flops 134316032 | bytes 8593408 | tf_op jit(solution)/shard_map/dot_general | solution.py:11
  223.5 0.1 fusion.2
  223.6 0.2 fusion
  223.9 0.0 copy-done.1
  223.9 0.9 convolution_add_fusion.3
  224.8 0.0 all-reduce.4.cloned.1.call-update
  224.8 2.4 all-reduce.8.cloned.1.call-done
  227.2 57.0 %all-reduce.6.cloned.1.call-done = f32[16,2048]{1,0:T(8,128)} async-done(((f32[16,2048]{1,0:T(8,128)}), f32[16,2048]{1,0:T(8,128)}) %all-reduce.6.cloned.1.call-update) | async-done | bytes 131088 | tf_op jit(solution)/shard_map/psum | solution.py:69
  284.2 1.6 multiply_add_fusion
  285.9 71.9 %all-reduce.4.cloned.1.call-done = f32[16,2048]{1,0:T(8,128)} async-done(((f32[16,2048]{1,0:T(8,128)}), f32[16,2048]{1,0:T(8,128)}) %all-reduce.4.cloned.1.call-update) | async-done | bytes 131088 | tf_op jit(solution)/shard_map/psum | solution.py:92
  357.8 1.6 copy.15
  (5 shorter events, 0.1 us)
Async XLA Ops:
  7.2 85.9 %copy-start = (bf16[16,2048]{1,0:T(8,128)(2,1)S(1)}, bf16[16,2048]{1,0:T(8,128)(2,1)}, u32[]{:S(2)}) copy-start(bf16[16,2048]{1,0:T(8,128)(2,1)} %param.9) | copy-start | bytes 196612
  7.2 85.9 %all-gather.2.cloned.1.call-start = ((), (), s32[]{:S(2)}) async-start(), calls=%async_computation.2 | async-start | bytes 5242880 | tf_op jit(solution)/shard_map/all_gather | solution.py:43
  7.9 192.0 %reduce-scatter.5.cloned.1.call-start = ((), (), s32[]{:S(2)}) async-start(), calls=%async_computation.4 | async-start | bytes 81920 | tf_op jit(solution)/shard_map/reduce_scatter | solution.py:48
  97.1 104.8 %reduce-scatter.3.cloned.1.call-start = ((), (), s32[]{:S(2)}) async-start(), calls=%async_computation.3 | async-start | bytes 10485760 | tf_op jit(solution)/shard_map/reduce_scatter | solution.py:47
  111.6 115.7 %all-reduce.8.cloned.1.call-start = ((), (), s32[]{:S(2)}) async-start(), calls=%async_computation.7 | async-start | bytes 262144 | tf_op jit(solution)/shard_map/psum | solution.py:50
  111.8 4.6 %copy-start.2 = (bf16[16,2048]{1,0:T(8,128)(2,1)S(1)}, bf16[16,2048]{1,0:T(8,128)(2,1)}, u32[]{:S(2)}) copy-start(bf16[16,2048]{1,0:T(8,128)(2,1)} %param.10) | copy-start | bytes 196612
  117.3 166.9 %all-reduce.6.cloned.1.call-start = ((), (), s32[]{:S(2)}) async-start(), calls=%async_computation.6 | async-start | bytes 262144 | tf_op jit(solution)/shard_map/psum | solution.py:69
  117.3 5.9 %copy-start.5 = (s32[1,8]{1,0:T(1,128)S(1)}, s32[1,8]{1,0:T(1,128)}, u32[]{:S(2)}) copy-start(s32[1,8]{1,0:T(1,128)} %param.13) | copy-start | bytes 100
  117.4 12.7 %copy-start.4 = (f32[2048]{0:T(1024)S(1)}, f32[2048]{0:T(1024)}, u32[]{:S(2)}) copy-start(f32[2048]{0:T(1024)} %param.11) | copy-start | bytes 24580
  117.4 12.8 %copy-start.3 = (bf16[256,2048]{1,0:T(8,128)(2,1)S(1)}, bf16[256,2048]{1,0:T(8,128)(2,1)}, u32[]{:S(2)}) copy-start(bf16[256,2048]{1,0:T(8,128)(2,1)} %param.12) | copy-start | bytes 3145732
  201.8 156.0 %all-reduce.4.cloned.1.call-start = ((), (), s32[]{:S(2)}) async-start(), calls=%async_computation.5 | async-start | bytes 262144 | tf_op jit(solution)/shard_map/psum | solution.py:92
  217.8 6.1 %copy-start.1 = (bf16[256,2048]{1,0:T(8,128)(2,1)S(1)}, bf16[256,2048]{1,0:T(8,128)(2,1)}, u32[]{:S(2)}) copy-start(bf16[256,2048]{1,0:T(8,128)(2,1)} %param.7) | copy-start | bytes 3145732
Sparse Core Ops, SparseCore 0:
  9.6 83.4 all-gather.1
  97.2 18.0 reduce-scatter.4
  117.9 75.6 reduce-scatter.2
  195.8 31.4 all-reduce.7
  230.7 53.4 all-reduce.5
  288.0 69.7 all-reduce.3
where the time goes:
time: 367 us; the launch traced here: 366 us
  waiting for transfers between devices  217 us (59%)
  blocking collectives  87.8 us (24%)
  matrix products  42.5 us (12%)
  between operations  14.3 us (4%)
    all_gather x1, waiting for transfers between devices, per_device(): portion = lax.all_gather(tokens, 'col', axis=0, tiled=True)  85.1 us
    psum x1, waiting for transfers between devices, per_device(): lax.psum(row_term + first_group * norm_term, ('dp', 'col'))  71.9 us
    psum x1, blocking collectives, per_device(): backward_rows = lax.psum(padded, ('row', 'col')).astype(jnp.bfloat16)  69.2 us
    psum x1, waiting for transfers between devices, per_device(): scale_grad, bgrad_data = lax.psum((scale_terms, bgrad_terms), ('dp', 'row'))  57 us
    dot_general x8, matrix products, contract_product(): lax.dot_general(left, right, (((left_dim,), (right_dim,)), ((), ())), pre...  19.1 us
    dot_general x1, matrix products, per_device(): jnp.dot(portion, frozen_weight, preferred_element_type=jnp.float32)  14.4 us
    psum x1, blocking collectives, per_device(): scale_grad, bgrad_data = lax.psum((scale_terms, bgrad_terms), ('dp', 'row'))  12.1 us
  transfers between devices with their start and end apart: 6, of which 4 were waited for; matrix products, arithmetic and copies ran while one was open for 11% of the time, Pallas kernels for 0%

commit v1 on v0

--- a/solution.py
+++ b/solution.py
@@ -1,3 +1,4 @@
+import functools
 import jax
 import jax.numpy as jnp
 from jax import lax
@@ -5,6 +6,15 @@
 
 norm_eps = 1e-06
 highest_precision = lax.Precision.HIGHEST
+
+
+def slots_begin(mat, net_axis, chip_axis):
+    for idx in (net_axis, chip_axis):
+        mat = lax.psum(mat, idx)
+    return mat
+
+
+step_on_stops_all = functools.partial(slots_begin, net_axis="col", chip_axis="row")
 
 
 def contract_product(left, right, left_dim, right_dim):
@@ -77,7 +87,7 @@
         row_index * block_rows,
         0,
     )
-    backward_rows = lax.psum(padded, ("row", "col")).astype(jnp.bfloat16)
+    backward_rows = step_on_stops_all(padded).astype(jnp.bfloat16)
     back_mine = lax.dynamic_slice_in_dim(backward_rows, col_index * local_rows, local_rows, 0)
     row_term = contract_product(back_mine, tokens, 0, 0)
     scaled_output_factor = (

time: 367 us -> 403 us (1.098)
  waiting for transfers between devices: 217 us -> 301 us
  blocking collectives: 87.8 us -> 38.3 us
    reduce_scatter x1, waiting for transfers between devices: 0.02 us -> 72 us  [per_device(): lax.psum_scatter(base_piece, 'row', scatter_dimension=0, tiled=True)]
    psum x1, blocking collectives: 69.2 us -> 17 us  [slots_begin(): mat = lax.psum(mat, idx)]
    all_gather x1, waiting for transfers between devices: 85.1 us -> 68.2 us  [per_device(): portion = lax.all_gather(tokens, 'col', axis=0, tiled=True)]
    psum x0 -> x1, waiting for transfers between devices: none -> 15.6 us  [slots_begin(): mat = lax.psum(mat, idx)]
    psum x1, waiting for transfers between devices: 2.4 us -> 10.2 us  [per_device(): lax.psum((norm_terms, merged_factor_terms), 'row')]
    reduce_scatter x1, waiting for transfers between devices: 0.02 us -> 5.41 us  [per_device(): lax.psum_scatter(down_portion, 'row', scatter_dimension=0, tiled=True)]
  transfers between devices with their start and end apart: 6 -> 7, of which waited for: 4 -> 7; matrix products, arithmetic and copies ran while one was open for 11% -> 11% of each run, Pallas kernels for 0% -> 0%
where the time goes in v1:
time: 403 us; the launch traced here: 402 us
  waiting for transfers between devices  301 us (75%)
  matrix products  42.6 us (11%)
  blocking collectives  38.3 us (10%)
  between operations  14.3 us (4%)
    psum x1, waiting for transfers between devices, per_device(): lax.psum(row_term + first_group * norm_term, ('dp', 'col'))  72.1 us
    reduce_scatter x1, waiting for transfers between devices, per_device(): lax.psum_scatter(base_piece, 'row', scatter_dimension=0, tiled=True)  72 us
    all_gather x1, waiting for transfers between devices, per_device(): portion = lax.all_gather(tokens, 'col', axis=0, tiled=True)  68.2 us
    psum x1, waiting for transfers between devices, per_device(): scale_grad, bgrad_data = lax.psum((scale_terms, bgrad_terms), ('dp', 'row'))  57 us
    dot_general x8, matrix products, contract_product(): lax.dot_general(left, right, (((left_dim,), (right_dim,)), ((), ())), pre...  19.2 us
    psum x1, blocking collectives, slots_begin(): mat = lax.psum(mat, idx)  17 us
    psum x1, waiting for transfers between devices, slots_begin(): mat = lax.psum(mat, idx)  15.6 us
    dot_general x1, matrix products, per_device(): jnp.dot(portion, frozen_weight, preferred_element_type=jnp.float32)  14.5 us
  transfers between devices with their start and end apart: 7, of which 7 were waited for; matrix products, arithmetic and copies ran while one was open for 11% of the time, Pallas kernels for 0%

profile of v1, /device:TPU:0, one launch (start us, length us, event | category | flops | bytes accessed | tf_op | source)
XLA Modules:
  0.0 402.4 jit_solution(1951940285349590185)
XLA Ops:
  7.2 0.0 copy-start
  7.2 0.0 all-gather.2.cloned.1.call-start
  7.2 0.7 all-gather.2.cloned.1.call-update
  7.9 0.0 all-reduce.5.cloned.1.call-start
  8.0 0.8 reduce-window.4
  8.8 0.0 copy-done
  8.8 0.0 copy-start.6
  8.8 0.0 copy-start.5
  8.8 0.0 copy-start.3
  8.8 0.0 copy-start.4
  8.8 5.9 %multiply_reduce_fusion = f32[2048]{0:T(1024)S(1)} fusion(bf16[2048,2048]{1,0:T(8,128)(2,1)} %param.8, bf16[16,2048]{1,0:T(8,128)(2,1)S(1)} %copy-done, bf16[16,2048]{1,0:T(8,128)(2,1)} %param.10), kind=kOutput, calls=%fused_computation | convolution fusion | flops 150992896 | bytes 8527872 | tf_op jit(solution)/shard_map/dot_general | solution.py:21
  14.7 8.5 %psum.49 = f32[2048]{0:T(1024)S(1)} all-reduce(f32[2048]{0:T(1024)S(1)} %multiply_reduce_fusion), channel_id=1, replica_groups=mesh['dp'=2,'row'=4,'col'=4] {'row'}, use_global_device_ids=true, to_apply=%region_3.0 | all-reduce | flops 2048 | bytes 16384 | tf_op jit(solution)/shard_map/psum | solution.py:60
  23.3 0.0 copy-done.6
  23.3 0.1 select_reduce_fusion
  23.4 0.0 copy-done.5
  23.5 0.0 copy-done.3
  23.5 0.0 copy-done.4
  23.5 0.5 convolution_dynamic-update-slice_fusion
  24.0 0.0 copy-start.2
  24.0 0.8 copy-done.2
  24.8 0.0 all-reduce.5.cloned.1.call-update
  24.8 0.0 reduce-scatter.5.cloned.1.call-start
  24.9 68.2 %all-gather.2.cloned.1.call-done = bf16[1024,2048]{1,0:T(8,128)(2,1)} async-done(((bf16[256,2048]{1,0:T(8,128)(2,1)}), bf16[1024,2048]{1,0:T(8,128)(2,1)}) %all-gather.2.cloned.1.call-update) | async-done | bytes 4194320 | tf_op jit(solution)/shard_map/all_gather | solution.py:53
  93.1 4.0 fusion.14
  97.1 0.0 reduce-scatter.5.cloned.1.call-update
  97.1 0.0 reduce-scatter.3.cloned.1.call-start
  97.1 14.5 %fusion.13 = f32[1024,2048]{1,0:T(8,128)} fusion(bf16[1024,2048]{1,0:T(8,128)(2,1)} %all-gather.2.cloned.1.call-done, bf16[2048,2048]{1,0:T(8,128)(2,1)} %param.8), kind=kOutput, calls=%fused_computation.32 | convolution fusion | flops 8589934592 | bytes 20971520 | tf_op jit(solution)/shard_map/dot_general | solution.py:54
  111.7 0.0 reduce-scatter.3.cloned.1.call-update
  111.7 0.0 all-reduce.11.cloned.1.call-start
  111.7 0.1 fusion.16
  111.9 4.6 %fusion.15 = f32[16,2048]{1,0:T(8,128)S(1)} fusion(bf16[16,2048]{1,0:T(8,128)(2,1)S(1)} %copy-done, bf16[2048,2048]{1,0:T(8,128)(2,1)} %param.8), kind=kOutput, calls=%fused_computation.34 | convolution fusion | flops 134217728 | bytes 8585216 | tf_op jit(solution)/shard_map/dot_general | solution.py:48
  116.5 0.8 convolution_add_fusion.1
  117.4 0.0 all-reduce.11.cloned.1.call-update
  117.4 0.0 all-reduce.9.cloned.1.call-start
  117.4 15.6 %all-reduce.5.cloned.1.call-done = f32[1024,16]{1,0:T(8,128)} async-done(((f32[1024,16]{1,0:T(8,128)}), f32[1024,16]{1,0:T(8,128)}) %all-reduce.5.cloned.1.call-update) | async-done | bytes 65552 | tf_op jit(solution)/shard_map/psum | solution.py:13
  133.1 17.0 %psum.52 = bf16[1024,16]{1,0:T(8,128)(2,1)S(1)} all-reduce(f32[1024,16]{1,0:T(8,128)} %all-reduce.5.cloned.1.call-done), channel_id=1, replica_groups=mesh['dp'=2,'row'=4,'col'=4] {'row'}, use_global_device_ids=true, to_apply=%region_9.10 | all-reduce | flops 16384 | bytes 98304 | tf_op jit(solution)/shard_map/psum | solution.py:13
  150.1 5.4 %reduce-scatter.5.cloned.1.call-done = f32[256,16]{0,1:T(8,128)} async-done(((f32[1024,16]{0,1:T(8,128)}), f32[256,16]{0,1:T(8,128)}) %reduce-scatter.5.cloned.1.call-update) | async-done | bytes 16400 | tf_op jit(solution)/shard_map/reduce_scatter | solution.py:58
  155.5 1.8 fusion.1
  157.3 0.0 all-reduce.9.cloned.1.call-update
  157.3 0.0 all-reduce.7.cloned.1.call-start
  157.4 72.0 %reduce-scatter.3.cloned.1.call-done = f32[256,2048]{1,0:T(8,128)} async-done(((f32[1024,2048]{1,0:T(8,128)}), f32[256,2048]{1,0:T(8,128)}) %reduce-scatter.3.cloned.1.call-update) | async-done | bytes 2097168 | tf_op jit(solution)/shard_map/reduce_scatter | solution.py:57
  229.4 3.2 multiply_reduce_fusion.1
  232.6 12.8 %psum.50 = f32[2048]{0:T(1024)S(1)} all-reduce(f32[2048]{0:T(1024)S(1)} %get-tuple-element.4), channel_id=1, replica_groups=mesh['dp'=2,'row'=4,'col'=4] {'dp','row'}, use_global_device_ids=true, to_apply=%region_7.8 | all-reduce | flops 2048 | bytes 16384 | tf_op jit(solution)/shard_map/psum | solution.py:79
  245.4 0.6 fusion.6
  246.0 0.0 copy-start.1
  246.0 5.7 %fusion.3 = f32[16,2048]{1,0:T(8,128)S(1)} fusion(bf16[2048,2048]{1,0:T(8,128)(2,1)} %param.8, bf16[16,2048]{1,0:T(8,128)(2,1)S(1)} %copy-done.3, f32[2048]{0:T(1024)S(1)} %get-tuple-element.6), kind=kOutput, calls=%fused_computation.16 | convolution fusion | flops 134316032 | bytes 8593408 | tf_op jit(solution)/shard_map/dot_general | solution.py:21
  251.7 0.1 fusion.2
  251.9 0.2 fusion
  252.1 0.0 copy-done.1
  252.1 0.9 convolution_add_fusion.3
  253.0 0.0 all-reduce.7.cloned.1.call-update
  253.1 10.2 %all-reduce.11.cloned.1.call-done = f32[16,2048]{1,0:T(8,128)} async-done(((f32[16,2048]{1,0:T(8,128)}), f32[16,2048]{1,0:T(8,128)}) %all-reduce.11.cloned.1.call-update) | async-done | bytes 131088 | tf_op jit(solution)/shard_map/psum | solution.py:60
  263.3 57.0 %all-reduce.9.cloned.1.call-done = f32[16,2048]{1,0:T(8,128)} async-done(((f32[16,2048]{1,0:T(8,128)}), f32[16,2048]{1,0:T(8,128)}) %all-reduce.9.cloned.1.call-update) | async-done | bytes 131088 | tf_op jit(solution)/shard_map/psum | solution.py:79
  320.3 1.6 multiply_add_fusion
  321.9 72.1 %all-reduce.7.cloned.1.call-done = f32[16,2048]{1,0:T(8,128)} async-done(((f32[16,2048]{1,0:T(8,128)}), f32[16,2048]{1,0:T(8,128)}) %all-reduce.7.cloned.1.call-update) | async-done | bytes 131088 | tf_op jit(solution)/shard_map/psum | solution.py:102
  394.0 1.6 copy.16
  (5 shorter events, 0.1 us)
Async XLA Ops:
  7.2 1.6 copy-start
  7.2 85.9 %all-gather.2.cloned.1.call-start = ((), (), s32[]{:S(2)}) async-start(), calls=%async_computation.2 | async-start | bytes 5242880 | tf_op jit(solution)/shard_map/all_gather | solution.py:53
  7.9 125.2 %all-reduce.5.cloned.1.call-start = ((), (), s32[]{:S(2)}) async-start(), calls=%async_computation.5 | async-start | bytes 1048576 | tf_op jit(solution)/shard_map/psum | solution.py:13
  8.8 14.5 %copy-start.6 = (s32[1,8]{1,0:T(1,128)S(1)}, s32[1,8]{1,0:T(1,128)}, u32[]{:S(2)}) copy-start(s32[1,8]{1,0:T(1,128)} %param.13) | copy-start | bytes 100
  8.8 14.6 %copy-start.5 = (f32[2048]{0:T(1024)S(1)}, f32[2048]{0:T(1024)}, u32[]{:S(2)}) copy-start(f32[2048]{0:T(1024)} %param.11) | copy-start | bytes 24580
  8.8 14.7 %copy-start.3 = (bf16[16,2048]{1,0:T(8,128)(2,1)S(1)}, bf16[16,2048]{1,0:T(8,128)(2,1)}, u32[]{:S(2)}) copy-start(bf16[16,2048]{1,0:T(8,128)(2,1)} %param.10) | copy-start | bytes 196612
  8.8 14.7 %copy-start.4 = (bf16[256,2048]{1,0:T(8,128)(2,1)S(1)}, bf16[256,2048]{1,0:T(8,128)(2,1)}, u32[]{:S(2)}) copy-start(bf16[256,2048]{1,0:T(8,128)(2,1)} %param.12) | copy-start | bytes 3145732
  24.0 0.8 copy-start.2
  24.8 130.7 %reduce-scatter.5.cloned.1.call-start = ((), (), s32[]{:S(2)}) async-start(), calls=%async_computation.4 | async-start | bytes 81920 | tf_op jit(solution)/shard_map/reduce_scatter | solution.py:58
  97.1 132.3 %reduce-scatter.3.cloned.1.call-start = ((), (), s32[]{:S(2)}) async-start(), calls=%async_computation.3 | async-start | bytes 10485760 | tf_op jit(solution)/shard_map/reduce_scatter | solution.py:57
  111.7 151.6 %all-reduce.11.cloned.1.call-start = ((), (), s32[]{:S(2)}) async-start(), calls=%async_computation.8 | async-start | bytes 262144 | tf_op jit(solution)/shard_map/psum | solution.py:60
  117.4 202.9 %all-reduce.9.cloned.1.call-start = ((), (), s32[]{:S(2)}) async-start(), calls=%async_computation.7 | async-start | bytes 262144 | tf_op jit(solution)/shard_map/psum | solution.py:79
  157.3 236.7 %all-reduce.7.cloned.1.call-start = ((), (), s32[]{:S(2)}) async-start(), calls=%async_computation.6 | async-start | bytes 262144 | tf_op jit(solution)/shard_map/psum | solution.py:102
  246.0 6.1 %copy-start.1 = (bf16[256,2048]{1,0:T(8,128)(2,1)S(1)}, bf16[256,2048]{1,0:T(8,128)(2,1)}, u32[]{:S(2)}) copy-start(bf16[256,2048]{1,0:T(8,128)(2,1)} %param.7) | copy-start | bytes 3145732
Sparse Core Ops, SparseCore 0:
  9.6 83.4 all-gather.1
  96.0 37.0 all-reduce.4
  136.1 19.3 reduce-scatter.4
  157.9 71.3 reduce-scatter.2
  231.5 31.7 all-reduce.10
  266.8 53.4 all-reduce.8
  324.2 69.7 all-reduce.6
